TPU v7x, 32 devices: a whole 2x2x4 slice. The times are simulated.
32 devices in a mesh: dp: 8 (over y, x, core), seq: 4 (over z).
Axes of the slice: x: 2, y: 2, z: 4, core: 2. Of those that a mesh axis runs over, the one named last changes fastest.
Arguments:
- tile_tokens: bfloat16 [8, 128, 3200], P('dp', 'seq'), may hold values from -6 to 6
- proj_weight: bfloat16 [3200, 8192], P('dp', 'seq')
- text_hidden: bfloat16 [8, 512, 8192], P('dp', 'seq'), may hold values from -6 to 6
- cotangent: bfloat16 [8, 512, 8192], P('dp', 'seq'), may hold values from -1.1953125 to 1.1953125
- norm_gain: float32 [8192], replicated, may hold values from 0.25 to 1.75
- placeholders: int32 [8, 128], P('dp'), may hold values from 0 to 511, as said below
- bucket_levels: int32 [8, 4, 3200], P('dp', 'seq'), may hold values from 2 to 16
- row_draws: float32 [8, 4, 3200], P('dp', 'seq'), may hold values from 0 to 1
- column_draws: float32 [8, 8192], P('dp', 'seq'), may hold values from 0 to 1
Outputs:
- weight_grad: float32 [3200, 8192], P('dp', 'seq')
- gain_grad: float32 [8192], replicated
Inputs may be any that keep to these rules, and one draw needn't show every extreme that they name: Each row is strictly increasing. Among the positions of one device's block of 128 positions stand at most 48 placeholders, and in every row some block holds exactly 48.
All inputs are finite; a program needn't handle non-finite values.
Results may differ from a plain program's by a relative error of at most 0.014.
Values may be sent and summed in bfloat16 or wider, within the bound.
No kernel may reach another device: no remote copies, remote signals or barrier semaphores. Data moves between devices by JAX's collectives and lax.ppermute only.
A program may use at most 64 MiB of HBM per device.

v0:
```python
import jax
import jax.numpy as jnp
from jax import lax
from jax.sharding import PartitionSpec as P

IMG_MOST = 48
EPSILON = 1e-06


def quantize(gradient, levels_now, rows_now, columns_now):
    bucket_norm = jnp.sqrt(jnp.sum(gradient * gradient, axis=1, keepdims=True) + EPSILON)
    step_count = levels_now.astype(jnp.float32)[:, None]
    offset = 0.25 + 0.25 * (rows_now[:, None] + columns_now[None, :])
    ratio = jnp.abs(gradient) / bucket_norm * step_count
    lower = jnp.floor(ratio)
    quantum = lower + jnp.clip(2.0 * (ratio - lower - offset) + 0.5, 0.0, 1.0)
    return jnp.sign(gradient) * bucket_norm * quantum / step_count


def on_device(
    tile_tokens,
    proj_weight,
    text_hidden,
    cotangent,
    norm_gain,
    placeholders,
    bucket_levels,
    row_draws,
    column_draws,
):
    seq_count = lax.axis_size("seq")
    seq_index = lax.axis_index("seq")
    replicas = lax.axis_size("dp")
    places = placeholders[0]
    image_total = places.shape[0]
    tok_rows = text_hidden.shape[1]
    model_width = text_hidden.shape[2]
    columns = proj_weight.shape[1]
    all_positions = tok_rows * seq_count
    zero_half = jnp.zeros((), jnp.bfloat16)
    own_text = text_hidden[0]
    own_cot = cotangent[0]
    gathered = lax.all_gather(tile_tokens[0], "seq", axis=0, tiled=True)
    patch_block = gathered
    embedded = jnp.dot(
        patch_block,
        lax.all_gather(proj_weight, "dp", axis=0, tiled=True),
        preferred_element_type=jnp.float32,
    ).astype(jnp.bfloat16)
    image_marks = jnp.zeros((all_positions,), jnp.int32).at[places].set(1)
    local_marks = lax.dynamic_slice_in_dim(image_marks, seq_index * tok_rows, tok_rows)
    is_image = local_marks[:, None] == 1
    owners = places // tok_rows
    owner_ids = jnp.arange(seq_count, dtype=jnp.int32)
    counts = jnp.sum((owners[:, None] == owner_ids[None, :]).astype(jnp.int32), axis=0)
    starts = jnp.cumsum(counts) - counts
    own_start = starts[seq_index]
    own_count = counts[seq_index]
    slot_ids = jnp.arange(IMG_MOST, dtype=jnp.int32)
    source_rows = jnp.clip(own_start + slot_ids, 0, image_total - 1)
    local_slots = jnp.clip(jnp.take(places, source_rows) - seq_index * tok_rows, 0, tok_rows - 1)
    slot_live = (slot_ids < own_count)[:, None]
    flat_index = owners * IMG_MOST + (
        jnp.arange(image_total, dtype=jnp.int32) - jnp.take(starts, owners)
    )
    outgoing = jnp.where(slot_live, jnp.take(own_cot, local_slots, axis=0), zero_half)
    returned = lax.all_to_all(outgoing[None], "seq", split_axis=2, concat_axis=0, tiled=True)
    image_cot = jnp.take(returned.reshape(-1, columns), flat_index, axis=0).astype(jnp.float32)
    emb_float = embedded.astype(jnp.float32)
    column_gain = lax.dynamic_slice_in_dim(norm_gain, seq_index * columns, columns)
    grad_in = image_cot * column_gain[None, :]
    squares, mixed = lax.psum(
        (jnp.sum(emb_float * emb_float, axis=1), jnp.sum(grad_in * emb_float, axis=1)), "seq"
    )
    inverse = lax.rsqrt(squares / model_width + EPSILON)[:, None]
    normed = emb_float * inverse
    emb_grad = ((grad_in - normed * (mixed[:, None] * inverse / model_width)) * inverse).astype(
        jnp.bfloat16
    )
    image_part = jnp.sum(image_cot * normed, axis=0)
    text_float = own_text.astype(jnp.float32)
    text_inverse = lax.rsqrt(jnp.mean(text_float * text_float, axis=1, keepdims=True) + EPSILON)
    text_terms = own_cot.astype(jnp.float32) * text_float * text_inverse
    text_part = jnp.sum(jnp.where(is_image, 0.0, text_terms), axis=0)
    placed_part = lax.dynamic_update_slice_in_dim(
        jnp.zeros((model_width,), jnp.float32), image_part, seq_index * columns, 0
    )
    gain_part = text_part + placed_part
    own_levels = bucket_levels[0, 0]
    own_row_draws = row_draws[0, 0]
    own_column_draws = column_draws[0]
    patch_block = gathered
    gradient = lax.dot_general(
        patch_block, emb_grad, (((0,), (0,)), ((), ())), preferred_element_type=jnp.float32
    )
    summed = lax.psum_scatter(
        quantize(gradient, own_levels, own_row_draws, own_column_draws).astype(jnp.bfloat16),
        "dp",
        scatter_dimension=0,
        tiled=True,
    ).astype(jnp.float32)
    gain_total = lax.psum(gain_part, ("dp", "seq"))
    return (summed / replicas, gain_total / replicas)


def solution(mesh):
    return jax.shard_map(
        on_device,
        mesh=mesh,
        in_specs=(
            P("dp", "seq", None),
            P("dp", "seq"),
            P("dp", "seq", None),
            P("dp", "seq", None),
            P(),
            P("dp", None),
            P("dp", "seq", None),
            P("dp", "seq", None),
            P("dp", "seq"),
        ),
        out_specs=(P("dp", "seq"), P()),
        check_vma=False,
    )
```

profile of v0, /device:TPU:0, one launch (start us, length us, event | category | flops | bytes accessed | tf_op | source)
XLA Modules:
  0.0 315.0 jit_solution(2458585537406789046)
XLA Ops:
  7.2 0.0 copy-start
  7.2 0.0 all-gather.3.cloned.1.call-start
  7.3 0.7 all-gather.3.cloned.1.call-update
  7.9 0.7 and_select_fusion.5
  8.6 0.1 convert_reduce_fusion.1
  8.7 0.2 reduce-window.9
  8.9 0.6 dynamic_slice.12
  9.5 0.7 fusion.34
  10.2 0.7 fusion.33
  10.9 1.4 gather_fusion
  12.3 0.7 fusion.31
  13.0 3.6 %gather_fusion.1 = bf16[48,8192]{1,0:T(8,128)(2,1)S(1)} fusion(bf16[128,8192]{1,0:T(8,128)(2,1)} %bitcast.74, s32[1024]{0:T(1024)S(1)} %pad_clamp_fusion.1), kind=kCustom, calls=%fused_computation.1 | custom fusion | bytes 1573056 | tf_op jit(solution)/shard_map/jit(_take)/gather | solution.py:66
  16.6 1.3 compare_and_fusion
  17.9 0.2 fusion.21
  18.1 6.8 %copy.22 = bf16[1,48,8192]{1,0,2:T(2,128)(2,1)} copy(bf16[1,48,8192]{2,1,0:T(8,128)(2,1)S(1)} %fusion.21) | data formatting | bytes 1572864 | tf_op jit(solution)/shard_map/jit(_where)/select_n | solution.py:66
  24.8 0.5 broadcast.575
  25.3 45.2 %reduce.4 = bf16[8192,48]{1,0:T(8,128)(2,1)S(1)} reduce(bf16[8192,1,48]{2,1,0:T(2,128)(2,1)} %bitcast.76, bf16[]{:T(256)} %broadcast.575), dimensions={1}, to_apply=%bitcast.63.reduce_sub_computation | reduce | bytes 1572866
  70.6 4.0 %reshape.423 = bf16[4,2,49152]{2,1,0:T(2,128)(2,1)} reshape(bf16[8192,48]{1,0:T(8,128)(2,1)S(1)} %reduce.4) | data formatting | bytes 1572864
  74.6 6.3 %all-to-all-start = ((bf16[4,2,49152]{2,1,0:T(2,128)(2,1)}), bf16[4,2,49152]{2,1,0:T(2,128)(2,1)S(1)}, u32[]{:S(2)}, u32[]{:S(2)}) async-start(bf16[4,2,49152]{2,1,0:T(2,128)(2,1)} %reshape.423), calls=%async_computation | async-start | bytes 1572864 | tf_op jit(solution)/shard_map/all_to_all | solution.py:67
  80.9 0.7 dynamic_slice.14
  81.7 2.6 compare_and_fusion.1
  84.4 30.7 %all-gather = bf16[1,128,3200]{2,1,0:T(8,128)(2,1)S(1)} all-gather(bf16[1,32,3200]{2,1,0:T(8,128)(2,1)S(1)} %copy-done.4), channel_id=2, replica_groups=mesh['dp'=8,'seq'=4] {'seq'}, dimensions={1}, use_global_device_ids=true | all-gather | bytes 1024000 | tf_op jit(solution)/shard_map/all_gather | solution.py:43
  115.0 4.6 %reshape.424 = bf16[8192,1,48]{2,1,0:T(2,128)(2,1)} reshape(bf16[4,2,49152]{2,1,0:T(2,128)(2,1)S(1)} %all-to-all-done) | data formatting | bytes 1572864
  119.6 8.1 %copy.23 = bf16[1,48,8192]{2,1,0:T(8,128)(2,1)S(1)} copy(bf16[1,48,8192]{1,0,2:T(2,128)(2,1)} %bitcast.77) | data formatting | bytes 1572864 | tf_op jit(solution)/shard_map/all_to_all | solution.py:67
  127.8 0.6 all_to_all.12
  128.4 0.4 copy.24
  128.8 0.9 gather_fusion.2
  129.8 0.0 all-gather.3.cloned.1.call-done
  129.8 7.1 %multiply_reduce_fusion.1 = (f32[128]{0:T(128)S(1)}, f32[128,2048]{1,0:T(8,128)S(1)}) fusion(bf16[3200,2048]{1,0:T(8,128)(2,1)} %all-gather.3.cloned.1.call-done, bf16[1,128,3200]{2,1,0:T(8,128)(2,1)S(1)} %all-gather), kind=kOutput, calls=%fused_computation.31 | convolution fusion | flops 1678770048 | bytes 14975488 | tf_op jit(solution)/shard_map/dot_general | solution.py:45
  136.8 0.0 copy-start.2
  136.9 11.1 %psum.21 = f32[128]{0:T(128)S(1)} all-reduce(f32[128]{0:T(128)S(1)} %get-tuple-element.22), channel_id=1, replica_groups=mesh['dp'=8,'seq'=4] {'seq'}, use_global_device_ids=true, to_apply=%region_3.4 | all-reduce | flops 128 | bytes 1024 | tf_op jit(solution)/shard_map/psum | solution.py:72
  148.0 0.4 fusion.17
  148.4 8.4 %psum.22 = f32[128]{0:T(128)S(1)} all-reduce(f32[128]{0:T(128)S(1)} %get-tuple-element.13), channel_id=1, replica_groups=mesh['dp'=8,'seq'=4] {'seq'}, use_global_device_ids=true, to_apply=%region_5.6 | all-reduce | flops 128 | bytes 1024 | tf_op jit(solution)/shard_map/psum | solution.py:72
  156.8 0.0 copy-start.7
  156.8 5.1 %multiply_reduce_fusion = (f32[3200]{0:T(1024)S(1)}, f32[2048,3200]{1,0:T(8,128)S(1)}) fusion(bf16[1,128,3200]{2,1,0:T(8,128)(2,1)S(1)} %all-gather, f32[128,2048]{1,0:T(8,128)} %copy-done.2, f32[128]{0:T(128)S(1)} %multiply_multiply_fusion, f32[128]{0:T(128)S(1)} %add_rsqrt_fusion.1, f32[2048]{0:T(1024)S(1)} %dynamic_slice.14, ...), kind=kOutput, calls=%fused_computation.12 | convolution fusion | flops 1692922752 | bytes 28628608 | tf_op jit(solution)/shard_map/dot_general | solution.py:93
  162.0 22.2 %fusion.6 = bf16[3200,2048]{0,1:T(8,128)(2,1)} fusion(f32[2048,3200]{1,0:T(8,128)S(1)} %get-tuple-element.25, f32[3200]{0:T(1024)S(1)} %convert_reduce_fusion, f32[2048]{0:T(1024)S(1)} %bitcast.79, f32[3200]{0:T(1024)S(1)} %reduce.2, f32[3200]{0:T(1024)S(1)} %add_sqrt_fusion), kind=kLoop, calls=%fused_computation.13 | loop fusion | flops 117964800 | bytes 39368192 | tf_op jit(solution)/shard_map/convert_element_type | solution.py:97
  184.1 18.3 %copy.26 = bf16[3200,2048]{1,0:T(8,128)(2,1)} copy(bf16[3200,2048]{0,1:T(8,128)(2,1)} %fusion.6) | data formatting | bytes 26214400
  202.5 0.0 reduce-scatter.4.cloned.1.call-update
  202.5 1.0 scatter_custom_fusion
  203.5 0.1 dynamic-slice_compare_fusion
  203.6 2.1 fusion.10
  205.7 2.6 fusion.9
  208.3 41.3 %psum.23 = f32[8192]{0:T(1024)S(1)} all-reduce(f32[8192]{0:T(1024)S(1)} %add_dynamic-update-slice_fusion), channel_id=1, replica_groups=mesh['dp'=8,'seq'=4] {'dp','seq'}, use_global_device_ids=true, to_apply=%region_12.13 | all-reduce | flops 8192 | bytes 65536 | tf_op jit(solution)/shard_map/psum | solution.py:102
  249.7 0.6 broadcast_multiply_fusion
  250.3 47.4 %reduce-scatter.4.cloned.1.call-done = bf16[400,2048]{1,0:T(8,128)(2,1)} async-done(((bf16[3200,2048]{1,0:T(8,128)(2,1)}), bf16[400,2048]{1,0:T(8,128)(2,1)}) %reduce-scatter.4.cloned.1.call-update) | async-done | bytes 1638416
  297.7 2.8 copy.27
  300.5 2.5 convert_multiply_fusion.2
  303.0 5.2 %copy.25 = f32[400,2048]{1,0:T(8,128)} copy(f32[400,2048]{0,1:T(8,128)} %convert_multiply_fusion.2) | data formatting | bytes 6553600
  (29 shorter events, 0.2 us)
Async XLA Ops:
  7.2 74.5 %copy-start = (s32[1,128]{1,0:T(1,128)S(1)}, s32[1,128]{1,0:T(1,128)}, u32[]{:S(2)}) copy-start(s32[1,128]{1,0:T(1,128)} %param.14) | copy-start | bytes 1540
  7.2 74.5 %copy-start.6 = (f32[1,1,3200]{2,1,0:T(1,128)S(1)}, f32[1,1,3200]{2,1,0:T(1,128)}, u32[]{:S(2)}) copy-start(f32[1,1,3200]{2,1,0:T(1,128)} %param.16) | copy-start | bytes 38404
  7.2 77.1 %copy-start.5 = (s32[1,1,3200]{2,1,0:T(1,128)S(1)}, s32[1,1,3200]{2,1,0:T(1,128)}, u32[]{:S(2)}) copy-start(s32[1,1,3200]{2,1,0:T(1,128)} %param.15) | copy-start | bytes 38404
  7.2 77.2 %copy-start.4 = (bf16[1,32,3200]{2,1,0:T(8,128)(2,1)S(1)}, bf16[1,32,3200]{2,1,0:T(8,128)(2,1)}, u32[]{:S(2)}) copy-start(bf16[1,32,3200]{2,1,0:T(8,128)(2,1)} %param.9) | copy-start | bytes 614404
  7.2 122.6 %all-gather.3.cloned.1.call-start = ((), (), s32[]{:S(2)}) async-start(), calls=%async_computation.2 | async-start | bytes 14745600 | tf_op jit(solution)/shard_map/all_gather | solution.py:47
  74.6 40.5 %all-to-all-start = ((bf16[4,2,49152]{2,1,0:T(2,128)(2,1)}), bf16[4,2,49152]{2,1,0:T(2,128)(2,1)S(1)}, u32[]{:S(2)}, u32[]{:S(2)}) async-start(bf16[4,2,49152]{2,1,0:T(2,128)(2,1)} %reshape.423), calls=%async_computation | async-start | bytes 1572864 | tf_op jit(solution)/shard_map/all_to_all | solution.py:67
  80.9 216.8 %reduce-scatter.4.cloned.1.call-start = ((), (), s32[]{:S(2)}) async-start(), calls=%async_computation.3 | async-start | bytes 14745600
  129.7 27.0 %copy-start.3 = (bf16[128,2048]{1,0:T(8,128)(2,1)}, bf16[128,2048]{1,0:T(8,128)(2,1)S(1)}, u32[]{:S(2)}) copy-start(bf16[128,2048]{1,0:T(8,128)(2,1)S(1)} %gather_fusion.2) | copy-start | bytes 1572868
  136.8 19.9 %copy-start.2 = (f32[128,2048]{1,0:T(8,128)}, f32[128,2048]{1,0:T(8,128)S(1)}, u32[]{:S(2)}) copy-start(f32[128,2048]{1,0:T(8,128)S(1)} %get-tuple-element.23) | copy-start | bytes 3145732
  156.8 5.2 %copy-start.7 = (f32[1,2048]{1,0:T(1,128)S(1)}, f32[1,2048]{1,0:T(1,128)}, u32[]{:S(2)}) copy-start(f32[1,2048]{1,0:T(1,128)} %param.17) | copy-start | bytes 24580
  202.5 3.2 %copy-start.1 = (bf16[1,128,8192]{2,1,0:T(8,128)(2,1)S(1)}, bf16[1,128,8192]{2,1,0:T(8,128)(2,1)}, u32[]{:S(2)}) copy-start(bf16[1,128,8192]{2,1,0:T(8,128)(2,1)} %param.12) | copy-start | bytes 6291460
Sparse Core Ops, SparseCore 0:
  9.9 76.9 all-gather.2
  202.6 95.0 reduce-scatter.3
where the time goes:
time: 316 us; the launch traced here: 315 us
  blocking collectives  91.5 us (29%)
  other arithmetic  82.2 us (26%)
  local copies, waits for them, and re-layouts  60.3 us (19%)
  waiting for transfers between devices  48.1 us (15%)
  between operations  14.3 us (5%)
  matrix products  12.2 us (4%)
  starting transfers between devices  6.39 us (2%)
    unnamed x3, waiting for transfers between devices  48.1 us
    unnamed x2, other arithmetic  45.3 us
    psum x1, blocking collectives, on_device(): gain_total = lax.psum(gain_part, ('dp', 'seq'))  41.3 us
    unnamed x22, local copies, waits for them, and re-layouts  35.4 us
    all_gather x1, blocking collectives, on_device(): gathered = lax.all_gather(tile_tokens[0], 'seq', axis=0, tiled=True)  30.7 us
    convert_element_type x1, other arithmetic, on_device(): quantize(gradient, own_levels, own_row_draws, own_column_draws)  22.2 us
    psum x2, blocking collectives, on_device(): lax.psum((jnp.sum(emb_float * emb_float, axis=1), jnp.sum(grad_in * emb_f...  19.5 us
    all_to_all x3, local copies, waits for them, and re-layouts, on_device(): lax.all_to_all(outgoing[None], 'seq', split_axis=2, concat_axis=0, tiled=...  9.14 us
  transfers between devices with their start and end apart: 3, of which 1 were waited for; matrix products, arithmetic and copies ran while one was open for 29% of the time, Pallas kernels for 0%

commit v1 on v0

--- a/solution.py
+++ b/solution.py
@@ -40,7 +40,16 @@
     zero_half = jnp.zeros((), jnp.bfloat16)
     own_text = text_hidden[0]
     own_cot = cotangent[0]
-    gathered = lax.all_gather(tile_tokens[0], "seq", axis=0, tiled=True)
+    f_next = tile_tokens[0]
+    count_all = lax.axis_size("seq")
+    state_next = [(tick - 1, tick) for tick in range(1, count_all)] + [(count_all - 1, 0)]
+    stack_in = [f_next]
+    for _ in range(count_all - 1):
+        f_next = lax.ppermute(f_next, axis_name="seq", perm=state_next)
+        stack_in += [f_next]
+    piece_now = jnp.concatenate([*reversed(stack_in)], axis=0)
+    res = lax.axis_index("seq")
+    gathered = jnp.roll(piece_now, (res + 1) * f_next.shape[0], 0)
     patch_block = gathered
     embedded = jnp.dot(
         patch_block,

time: 316 us -> 340 us (1.076)
  blocking collectives: 91.5 us -> 57.5 us
  waiting for transfers between devices: 48.1 us -> 77.9 us
  local copies, waits for them, and re-layouts: 60.3 us -> 69.4 us
  matrix products: 12.2 us -> 20.7 us
  other arithmetic: 82.2 us -> 87.9 us
  starting transfers between devices: 6.39 us -> 10.4 us
    all_gather x1 -> x0, blocking collectives: 30.7 us -> none  [on_device(): gathered = lax.all_gather(tile_tokens[0], 'seq', axis=0, tiled=True)]
    ppermute x0 -> x3, waiting for transfers between devices: none -> 29.1 us  [on_device(): f_next = lax.ppermute(f_next, axis_name='seq', perm=state_next)]
    dot_general x1, matrix products: 5.14 us -> 13.7 us  [on_device(): lax.dot_general(patch_block, emb_grad, (((0,), (0,)), ((), ())), preferre...]
    unnamed x22 -> x25, local copies, waits for them, and re-layouts: 35.4 us -> 41.4 us
    ppermute x0 -> x3, starting transfers between devices: none -> 3.94 us  [on_device(): f_next = lax.ppermute(f_next, axis_name='seq', perm=state_next)]
  transfers between devices with their start and end apart: 3 -> 6, of which waited for: 1 -> 4; matrix products, arithmetic and copies ran while one was open for 29% -> 30% of each run, Pallas kernels for 0% -> 0%
where the time goes in v1:
time: 340 us; the launch traced here: 338 us
  other arithmetic  87.9 us (26%)
  waiting for transfers between devices  77.9 us (23%)
  local copies, waits for them, and re-layouts  69.4 us (20%)
  blocking collectives  57.5 us (17%)
  matrix products  20.7 us (6%)
  between operations  14.2 us (4%)
  starting transfers between devices  10.4 us (3%)
    unnamed x3, waiting for transfers between devices  48.8 us
    unnamed x2, other arithmetic  46.6 us
    unnamed x25, local copies, waits for them, and re-layouts  41.4 us
    psum x1, blocking collectives, on_device(): gain_total = lax.psum(gain_part, ('dp', 'seq'))  38.7 us
    ppermute x3, waiting for transfers between devices, on_device(): f_next = lax.ppermute(f_next, axis_name='seq', perm=state_next)  29.1 us
    convert_element_type x1, other arithmetic, on_device(): quantize(gradient, own_levels, own_row_draws, own_column_draws)  24.2 us
    psum x2, blocking collectives, on_device(): lax.psum((jnp.sum(emb_float * emb_float, axis=1), jnp.sum(grad_in * emb_f...  18.8 us
    dot_general x1, matrix products, on_device(): lax.dot_general(patch_block, emb_grad, (((0,), (0,)), ((), ())), preferre...  13.7 us
  transfers between devices with their start and end apart: 6, of which 4 were waited for; matrix products, arithmetic and copies ran while one was open for 30% of the time, Pallas kernels for 0%

profile of v1, /device:TPU:0, one launch (start us, length us, event | category | flops | bytes accessed | tf_op | source)
XLA Modules:
  0.0 338.0 jit_solution(2211481303170452609)
XLA Ops:
  7.2 0.7 all-gather.2.cloned.1.call-update
  7.9 0.7 and_select_fusion.5
  9.5 0.7 fusion.36
  10.2 0.7 fusion.33
  10.8 1.4 gather_fusion
  12.3 0.7 fusion.31
  13.0 1.0 gather_fusion.1
  14.0 1.3 compare_and_fusion
  15.3 1.0 fusion.18
  16.3 8.9 %copy.22 = bf16[1,48,8192]{1,0,2:T(2,128)(2,1)} copy(bf16[1,48,8192]{2,1,0:T(8,128)(2,1)} %fusion.18) | data formatting | bytes 1572864 | tf_op jit(solution)/shard_map/jit(_where)/select_n | solution.py:75
  25.8 46.6 %reduce.3 = bf16[8192,48]{1,0:T(8,128)(2,1)} reduce(bf16[8192,1,48]{2,1,0:T(2,128)(2,1)} %bitcast.62, bf16[]{:T(256)} %broadcast.573), dimensions={1}, to_apply=%bitcast.53.reduce_sub_computation | reduce | bytes 1572866
  72.4 5.1 %reshape.422 = bf16[4,2,49152]{2,1,0:T(2,128)(2,1)} reshape(bf16[8192,48]{1,0:T(8,128)(2,1)} %reduce.3) | data formatting | bytes 1572864
  77.5 6.4 %all-to-all-start = ((bf16[4,2,49152]{2,1,0:T(2,128)(2,1)}), bf16[4,2,49152]{2,1,0:T(2,128)(2,1)S(1)}, u32[]{:S(2)}, u32[]{:S(2)}) async-start(bf16[4,2,49152]{2,1,0:T(2,128)(2,1)} %reshape.422), calls=%async_computation | async-start | bytes 1572864 | tf_op jit(solution)/shard_map/all_to_all | solution.py:76
  83.9 2.0 collective-permute-start
  85.9 0.7 dynamic_slice.19
  86.7 2.6 compare_and_fusion.1
  89.3 16.0 %collective-permute-done = bf16[32,3200]{1,0:T(8,128)(2,1)S(1)} collective-permute-done((bf16[32,3200]{1,0:T(8,128)(2,1)S(1)}, bf16[32,3200]{1,0:T(8,128)(2,1)S(1)}, u32[]{:S(2)}, u32[]{:S(2)}) %collective-permute-start) | collective-permute-done | bytes 204832 | tf_op jit(solution)/shard_map/ppermute | solution.py:48
  105.3 1.9 collective-permute-start.1
  107.1 5.7 %collective-permute-done.1 = bf16[32,3200]{1,0:T(8,128)(2,1)S(1)} collective-permute-done((bf16[32,3200]{1,0:T(8,128)(2,1)S(1)}, bf16[32,3200]{1,0:T(8,128)(2,1)S(1)}, u32[]{:S(2)}, u32[]{:S(2)}) %collective-permute-start.1) | collective-permute-done | bytes 204832 | tf_op jit(solution)/shard_map/ppermute | solution.py:48
  112.9 7.4 %collective-permute-done.2 = bf16[32,3200]{1,0:T(8,128)(2,1)S(1)} collective-permute-done((bf16[32,3200]{1,0:T(8,128)(2,1)S(1)}, bf16[32,3200]{1,0:T(8,128)(2,1)S(1)}, u32[]{:S(2)}, u32[]{:S(2)}) %collective-permute-start.2) | collective-permute-done | bytes 204832 | tf_op jit(solution)/shard_map/ppermute | solution.py:48
  120.4 0.7 constant_dynamic-update-slice_fusion.7
  121.1 0.7 constant_dynamic-update-slice_fusion.6
  121.8 0.7 constant_dynamic-update-slice_fusion.5
  122.5 0.7 constant_dynamic-update-slice_fusion.4
  123.2 0.7 constant_dynamic-update-slice_fusion.3
  123.8 0.7 constant_dynamic-update-slice_fusion.2
  124.5 0.7 constant_dynamic-update-slice_fusion.1
  125.2 0.7 constant_dynamic-update-slice_fusion
  125.9 4.6 %reshape.423 = bf16[8192,1,48]{2,1,0:T(2,128)(2,1)} reshape(bf16[4,2,49152]{2,1,0:T(2,128)(2,1)S(1)} %all-to-all-done) | data formatting | bytes 1572864
  130.5 8.1 %copy.23 = bf16[1,48,8192]{2,1,0:T(8,128)(2,1)S(1)} copy(bf16[1,48,8192]{1,0,2:T(2,128)(2,1)} %bitcast.63) | data formatting | bytes 1572864 | tf_op jit(solution)/shard_map/all_to_all | solution.py:76
  138.7 1.5 all_to_all.12
  140.2 1.6 copy.24
  141.8 1.7 gather_fusion.2
  143.5 7.0 %multiply_reduce_fusion.1 = (f32[128]{0:T(128)S(1)}, f32[128,2048]{1,0:T(8,128)S(1)}) fusion(bf16[3200,2048]{1,0:T(8,128)(2,1)} %all-gather.2.cloned.1.call-done, bf16[256,3200]{1,0:T(8,128)(2,1)} %constant_dynamic-update-slice_fusion, s32[]{:T(128)S(6)} %select_n.196), kind=kOutput, calls=%fused_computation.31 | convolution fusion | flops 1678770048 | bytes 14975492 | tf_op jit(solution)/shard_map/dot_general | solution.py:54
  150.5 8.4 %psum.21 = f32[128]{0:T(128)S(1)} all-reduce(f32[128]{0:T(128)S(1)} %get-tuple-element.22), channel_id=1, replica_groups=mesh['dp'=8,'seq'=4] {'seq'}, use_global_device_ids=true, to_apply=%region_3.4 | all-reduce | flops 128 | bytes 1024 | tf_op jit(solution)/shard_map/psum | solution.py:81
  158.9 1.5 fusion.17
  160.4 10.3 %psum.22 = f32[128]{0:T(128)S(1)} all-reduce(f32[128]{0:T(128)S(1)} %get-tuple-element.13), channel_id=1, replica_groups=mesh['dp'=8,'seq'=4] {'seq'}, use_global_device_ids=true, to_apply=%region_5.6 | all-reduce | flops 128 | bytes 1024 | tf_op jit(solution)/shard_map/psum | solution.py:81
  170.7 13.7 %multiply_reduce_fusion = (f32[3200]{0:T(1024)S(1)}, f32[3200,2048]{0,1:T(8,128)}) fusion(f32[128,2048]{1,0:T(8,128)S(1)} %get-tuple-element.23, f32[128]{0:T(128)S(1)} %multiply_multiply_fusion, f32[128]{0:T(128)S(1)} %add_rsqrt_fusion.1, f32[2048]{0:T(1024)S(1)} %dynamic_slice.19, bf16[128,2048]{1,0:T(8,128)(2,1)} %gather_fusion.2, ...), kind=kOutput, calls=%fused_computation.12 | convolution fusion | flops 1692922752 | bytes 28628612 | tf_op jit(solution)/shard_map/dot_general | solution.py:102
  184.5 24.2 %fusion.6 = bf16[3200,2048]{0,1:T(8,128)(2,1)} fusion(f32[3200,2048]{0,1:T(8,128)} %get-tuple-element.25, f32[2048]{0:T(1024)S(1)} %bitcast.66, f32[3200]{0:T(1024)S(1)} %reduce.1, f32[3200]{0:T(1024)S(1)} %convert_reduce_fusion, f32[3200]{0:T(1024)S(1)} %add_sqrt_fusion), kind=kLoop, calls=%fused_computation.13 | loop fusion | flops 117964800 | bytes 39368192 | tf_op jit(solution)/shard_map/convert_element_type | solution.py:106
  208.6 18.3 %copy.26 = bf16[3200,2048]{1,0:T(8,128)(2,1)} copy(bf16[3200,2048]{0,1:T(8,128)(2,1)} %fusion.6) | data formatting | bytes 26214400
  227.0 1.0 scatter_custom_fusion
  228.1 2.1 fusion.10
  230.2 3.1 fusion.9
  233.2 38.7 %psum.23 = f32[8192]{0:T(1024)S(1)} all-reduce(f32[8192]{0:T(1024)S(1)} %add_dynamic-update-slice_fusion), channel_id=1, replica_groups=mesh['dp'=8,'seq'=4] {'dp','seq'}, use_global_device_ids=true, to_apply=%region_12.13 | all-reduce | flops 8192 | bytes 65536 | tf_op jit(solution)/shard_map/psum | solution.py:111
  272.6 48.1 %reduce-scatter.4.cloned.1.call-done = bf16[400,2048]{1,0:T(8,128)(2,1)} async-done(((bf16[3200,2048]{1,0:T(8,128)(2,1)}), bf16[400,2048]{1,0:T(8,128)(2,1)}) %reduce-scatter.4.cloned.1.call-update) | async-done | bytes 1638416
  320.7 2.8 copy.27
  323.5 2.5 convert_multiply_fusion.2
  326.0 5.2 %copy.25 = f32[400,2048]{1,0:T(8,128)} copy(f32[400,2048]{0,1:T(8,128)} %convert_multiply_fusion.2) | data formatting | bytes 6553600
  (38 shorter events, 2.5 us)
Async XLA Ops:
  7.2 5.8 %copy-start.1 = (bf16[1,128,8192]{2,1,0:T(8,128)(2,1)S(1)}, bf16[1,128,8192]{2,1,0:T(8,128)(2,1)}, u32[]{:S(2)}) copy-start(bf16[1,128,8192]{2,1,0:T(8,128)(2,1)} %param.12) | copy-start | bytes 6291460
  7.2 136.3 %all-gather.2.cloned.1.call-start = ((), (), s32[]{:S(2)}) async-start(), calls=%async_computation.2 | async-start | bytes 14745600 | tf_op jit(solution)/shard_map/all_gather | solution.py:56
  25.8 58.1 %copy-start.2 = (bf16[1,32,3200]{2,1,0:T(8,128)(2,1)S(1)}, bf16[1,32,3200]{2,1,0:T(8,128)(2,1)}, u32[]{:S(2)}) copy-start(bf16[1,32,3200]{2,1,0:T(8,128)(2,1)} %param.9) | copy-start | bytes 614404
  25.8 60.8 %copy-start.4 = (f32[1,1,3200]{2,1,0:T(1,128)S(1)}, f32[1,1,3200]{2,1,0:T(1,128)}, u32[]{:S(2)}) copy-start(f32[1,1,3200]{2,1,0:T(1,128)} %param.16) | copy-start | bytes 38404
  25.8 60.9 %copy-start = (s32[1,128]{1,0:T(1,128)S(1)}, s32[1,128]{1,0:T(1,128)}, u32[]{:S(2)}) copy-start(s32[1,128]{1,0:T(1,128)} %param.14) | copy-start | bytes 1540
  25.8 87.1 %copy-start.3 = (s32[1,1,3200]{2,1,0:T(1,128)S(1)}, s32[1,1,3200]{2,1,0:T(1,128)}, u32[]{:S(2)}) copy-start(s32[1,1,3200]{2,1,0:T(1,128)} %param.15) | copy-start | bytes 38404
  77.5 48.4 %all-to-all-start = ((bf16[4,2,49152]{2,1,0:T(2,128)(2,1)}), bf16[4,2,49152]{2,1,0:T(2,128)(2,1)S(1)}, u32[]{:S(2)}, u32[]{:S(2)}) async-start(bf16[4,2,49152]{2,1,0:T(2,128)(2,1)} %reshape.422), calls=%async_computation | async-start | bytes 1572864 | tf_op jit(solution)/shard_map/all_to_all | solution.py:76
  83.9 236.8 %reduce-scatter.4.cloned.1.call-start = ((), (), s32[]{:S(2)}) async-start(), calls=%async_computation.3 | async-start | bytes 14745600
  83.9 21.4 %collective-permute-start = (bf16[32,3200]{1,0:T(8,128)(2,1)S(1)}, bf16[32,3200]{1,0:T(8,128)(2,1)S(1)}, u32[]{:S(2)}, u32[]{:S(2)}) collective-permute-start(bf16[32,3200]{1,0:T(8,128)(2,1)S(1)} %bitcast.65), channel_id=1, source_target_pairs={{0,1},{1,2},{2,3},{3,0},{4,5},{5,6},{6,7},{7,4},{8,9},{9,10},{10,1... | collective-permute-start | bytes 614408 | tf_op jit(solution)/shard_map/ppermute | solution.py:48
  105.3 7.6 %collective-permute-start.1 = (bf16[32,3200]{1,0:T(8,128)(2,1)S(1)}, bf16[32,3200]{1,0:T(8,128)(2,1)S(1)}, u32[]{:S(2)}, u32[]{:S(2)}) collective-permute-start(bf16[32,3200]{1,0:T(8,128)(2,1)S(1)} %collective-permute-done), channel_id=1, source_target_pairs={{0,1},{1,2},{2,3},{3,0},{4,5},{5,6},{6,7},{7,4},{8,9},{9,10},{10,1... | collective-permute-start | bytes 614408 | tf_op jit(solution)/shard_map/ppermute | solution.py:48
  112.8 7.6 %collective-permute-start.2 = (bf16[32,3200]{1,0:T(8,128)(2,1)S(1)}, bf16[32,3200]{1,0:T(8,128)(2,1)S(1)}, u32[]{:S(2)}, u32[]{:S(2)}) collective-permute-start(bf16[32,3200]{1,0:T(8,128)(2,1)S(1)} %collective-permute-done.1), channel_id=1, source_target_pairs={{0,1},{1,2},{2,3},{3,0},{4,5},{5,6},{6,7},{7,4},{8,9},{9,10},{10,1... | collective-permute-start | bytes 614408 | tf_op jit(solution)/shard_map/ppermute | solution.py:48
  170.7 13.7 %copy-start.5 = (f32[1,2048]{1,0:T(1,128)S(1)}, f32[1,2048]{1,0:T(1,128)}, u32[]{:S(2)}) copy-start(f32[1,2048]{1,0:T(1,128)} %param.17) | copy-start | bytes 24580
Sparse Core Ops, SparseCore 0:
  9.9 76.9 all-gather.1
  227.1 93.5 reduce-scatter.3
